TPU v7x, 32 devices: a whole 2x2x4 slice. The times are simulated.
32 devices in a mesh: gx: 8 (over z, y), gy: 4 (over x, core).
Axes of the slice: x: 2, y: 2, z: 4, core: 2. Of those that a mesh axis runs over, the one named last changes fastest.
Arguments:
- modes: float32 [2, 3, 96, 64, 128], P(None, None, 'gx', 'gy'), may hold values from -6 to 6
- moduli: float32 [96, 64, 128], P('gx', 'gy'), may hold values from 0.5 to 2
- pinned: int32 [96, 64, 128], P('gx', 'gy'), may hold values 0 or 1
- spectrum: float32 [3, 2], replicated, may hold values from 0.175 to 5, as said below
Outputs:
- correction: float32 [2, 3, 96, 64, 128], P(None, None, 'gx', 'gy')
Inputs may be any that keep to these rules, and one draw needn't show every extreme that they name: spectrum[l] = (lower, upper) with upper from 3.5 to 5 and lower 0.05 to 0.15 times upper.
All inputs are finite; a program needn't handle non-finite values. No bound on the sum of `pinned` on one device may be relied on, other than what follows from the above.
Results may differ from a plain program's by a relative error of at most 0.0003.
Values sent between devices are 32-bit elements; how exact they have to be, the bound alone decides.
A program may use at most 128 MiB of HBM per device.

v0:
```python
import jax
import jax.numpy as jnp
import numpy as np
from jax import lax
from jax.sharding import PartitionSpec as P

DEG = 3
COARSE_DEG = 4


MU_SHEAR = 1.0
LAMBDA_BULK = 1.5
PROLONG_TABLES = {
    4: np.array(
        [[1.0, 0.0, 0.0], [0.375, 0.75, -0.125], [0.0, 1.0, 0.0], [-0.125, 0.75, 0.375]],
        dtype=np.float32,
    ),
    2: np.array([[1.0, 0.0], [0.5, 0.5]], dtype=np.float32),
}
GAUSS_POINTS = [
    -0.9602898564975363,
    -0.7966664774136267,
    -0.525532409916329,
    -0.1834346424956498,
    0.1834346424956498,
    0.525532409916329,
    0.7966664774136267,
    0.9602898564975363,
]
GAUSS_WEIGHTS = [
    0.1012285362903763,
    0.2223810344533745,
    0.3137066458778873,
    0.362683783378362,
    0.362683783378362,
    0.3137066458778873,
    0.2223810344533745,
    0.1012285362903763,
]


def padded_2(cells, sides, width):
    for axis, dim in sides:
        count = lax.axis_size(axis)
        ends = count - 1
        head = lax.slice_in_dim(cells, 0, width, axis=dim)
        tail = lax.slice_in_dim(cells, cells.shape[dim] - width, cells.shape[dim], axis=dim)
        cells = jnp.concatenate(
            [
                lax.ppermute(tail, axis, [(i, (i + 1) % count) for i in range(ends)]),
                cells,
                lax.ppermute(head, axis, [((i + 1) % count, i) for i in range(ends)]),
            ],
            axis=dim,
        )
    return cells


def passed_along(value, axis, by):
    size = lax.axis_size(axis)
    pairs = [(i, i + by) for i in range(size) if 0 <= i + by < size]
    return lax.ppermute(value, axis, pairs)


def assemble(element, degree):
    coef_table = np.zeros((degree, 2 * degree + 1))
    for residue in range(degree):
        for offset in range(-degree, degree + 1):
            target = residue + offset
            if 0 <= target <= degree:
                coef_table[residue, offset + degree] += element[residue, target]
            if residue == 0 and offset <= 0:
                coef_table[residue, offset + degree] += element[degree, degree + offset]
    return coef_table.astype(np.float32)


def basis_tables(degree):
    nodes = [float(place) / degree for place in range(degree + 1)]
    points = 0.5 * (np.array(GAUSS_POINTS) + 1.0)
    weights = 0.5 * np.array(GAUSS_WEIGHTS)
    values = np.zeros((degree + 1, points.size))
    slopes = np.zeros((degree + 1, points.size))
    for column in range(degree + 1):
        product = np.ones(points.size)
        for other in range(degree + 1):
            if other != column:
                product = product * (points - nodes[other]) / (nodes[column] - nodes[other])
        values[column] = product
        slope_sum = np.zeros(points.size)
        for skipped in range(degree + 1):
            if skipped != column:
                partial_prod = np.ones(points.size) / (nodes[column] - nodes[skipped])
                for other in range(degree + 1):
                    if other != column and other != skipped:
                        partial_prod = (
                            partial_prod * (points - nodes[other]) / (nodes[column] - nodes[other])
                        )
                slope_sum = slope_sum + partial_prod
        slopes[column] = slope_sum
    mass_el = values * weights @ values.T
    stiff_el = slopes * weights @ slopes.T
    mixed_el = slopes * weights @ values.T
    return [
        assemble(mass_el, degree),
        assemble(stiff_el, degree),
        assemble(mixed_el, degree),
        assemble(mixed_el.T, degree),
    ]


def coupling():
    return MU_SHEAR + (LAMBDA_BULK + MU_SHEAR) * np.eye(3, dtype=np.float32)


def line_apply(field, along, coef_table, margin):
    degree = coef_table.shape[0]
    length = field.shape[along] - 2 * degree
    residue = (np.arange(length) + degree - margin) % degree
    coef_rows = coef_table[residue]
    shape_out = [1] * field.ndim
    shape_out[along] = length
    summed = None
    for offset in range(2 * degree + 1):
        window = lax.slice_in_dim(field, offset, offset + length, 1, along)
        weighted = window * jnp.asarray(coef_rows[:, offset].reshape(shape_out))
        summed = weighted if summed is None else summed + weighted
    return summed


def z_line(field, coef_table):
    degree = coef_table.shape[0]
    widths = [(0, 0)] * (field.ndim - 1) + [(degree, degree)]
    return line_apply(jnp.pad(field, widths), field.ndim - 1, coef_table, degree)


def elastic(padded, tables, margin):
    mass_tab, stiff_tab, mixed_tab, trans_tab = tables
    weights = coupling()
    z_mass = z_line(padded, mass_tab)
    z_stiff = z_line(padded, stiff_tab)
    along_x = line_apply(line_apply(z_mass, 3, mass_tab, margin), 2, stiff_tab, margin)
    along_y = line_apply(line_apply(z_mass, 3, stiff_tab, margin), 2, mass_tab, margin)
    along_z = line_apply(line_apply(z_stiff, 3, mass_tab, margin), 2, mass_tab, margin)
    outputs = []
    for target in range(3):
        result = (
            weights[target, 0] * along_x[:, target]
            + weights[target, 1] * along_y[:, target]
            + weights[target, 2] * along_z[:, target]
        )
        for source in range(3):
            if source != target:
                chosen = [mass_tab, mass_tab, mass_tab]
                chosen[target] = mixed_tab
                chosen[source] = trans_tab
                coupled = z_line(padded[:, source], chosen[2])
                coupled = line_apply(coupled, 2, chosen[1], margin)
                coupled = line_apply(coupled, 1, chosen[0], margin)
                result = result + (LAMBDA_BULK + MU_SHEAR) * coupled
        outputs.append(result)
    return jnp.stack(outputs, 1)


def level_fields(moduli, pinned, stride):
    sampled = moduli[::stride, ::stride, ::stride]
    pinned_f = pinned[::stride, ::stride, ::stride].astype(jnp.float32)
    return (sampled * (1.0 - pinned_f), pinned_f)


def inverse_diag(scaling, pinned_f, tables):
    mass_tab, stiff_tab = (tables[0], tables[1])
    degree = mass_tab.shape[0]
    weights = coupling()
    centers = []
    for along in range(3):
        residue = np.arange(scaling.shape[along]) % degree
        shape_out = [1, 1, 1]
        shape_out[along] = scaling.shape[along]
        centers.append(
            (
                mass_tab[residue, degree].reshape(shape_out),
                stiff_tab[residue, degree].reshape(shape_out),
            )
        )
    rows_out = []
    for target in range(3):
        diagonal = weights[target, 0] * centers[0][1] * centers[1][0] * centers[2][0]
        diagonal = diagonal + weights[target, 1] * centers[0][0] * centers[1][1] * centers[2][0]
        diagonal = diagonal + weights[target, 2] * centers[0][0] * centers[1][0] * centers[2][1]
        rows_out.append(scaling * scaling * jnp.asarray(diagonal) + pinned_f)
    return 1.0 / jnp.stack(rows_out, 0)


def operate(field, scaling, pinned_f, tables, padder):
    degree = tables[0].shape[0]
    padded = padder(scaling * field, degree)
    return scaling * elastic(padded, tables, degree) + pinned_f * field


def chebyshev(source, initial, n_steps, bounds, inverse, apply_op):
    low_end = bounds[0]
    top_end = bounds[1]
    center = 0.5 * (top_end + low_end)
    radius = 0.5 * (top_end - low_end)
    ratio_cs = center / radius
    rho_now = 1.0 / ratio_cs
    residual = source if initial is None else source - apply_op(initial)
    update = inverse * residual / center
    solution = update if initial is None else initial + update
    for sweep_at in range(n_steps - 1):
        residual = residual - apply_op(update)
        rho_next = 1.0 / (2.0 * ratio_cs - rho_now)
        update = rho_next * rho_now * update + 2.0 * rho_next / radius * inverse * residual
        solution = solution + update
        rho_now = rho_next
    return solution


def alternate(pieces, along):
    stacked = jnp.stack(pieces, along + 1)
    dims_now = list(stacked.shape)
    merged = dims_now[:along] + [dims_now[along] * dims_now[along + 1]] + dims_now[along + 2 :]
    return stacked.reshape(merged)


def restrict_line(field, along, table, margin):
    period, tap_count = table.shape
    half_per = period // 2
    owned_n = field.shape[along] - 2 * margin
    widths = [(0, 0)] * field.ndim
    widths[along] = (period - margin, 0)
    field = jnp.pad(field, widths)
    start_at = 0
    blocks = lax.slice_in_dim(field, start_at, start_at + owned_n + period, 1, along)
    dims_now = list(blocks.shape)
    elems = owned_n // period
    blocks = blocks.reshape(dims_now[:along] + [elems + 1, period] + dims_now[along + 1 :])
    tap_sums = []
    for tap_at in range(tap_count):
        running = None
        for residue in range(period):
            if table[residue, tap_at] != 0.0:
                portion = float(table[residue, tap_at]) * lax.index_in_dim(
                    blocks, residue, along + 1, False
                )
                running = portion if running is None else running + portion
        tap_sums.append(running)
    leading = lax.slice_in_dim(tap_sums[0], 1, elems + 1, 1, along) + lax.slice_in_dim(
        tap_sums[half_per], 0, elems, 1, along
    )
    pieces = [leading] + [
        lax.slice_in_dim(tap_sums[tap_at], 1, elems + 1, 1, along) for tap_at in range(1, half_per)
    ]
    return alternate(pieces, along)


def restrict_all(field, margin, degree):
    table = PROLONG_TABLES[degree]
    coarse = restrict_line(field, 2, table, margin)
    coarse = restrict_line(coarse, 3, table, margin)
    return restrict_line(coarse, 4, table, 0)


def prolong_line(field, along, table, margin):
    period, tap_count = table.shape
    half_per = period // 2
    elems = (field.shape[along] - 2 * margin) // half_per
    columns = [
        lax.slice_in_dim(
            field, margin + tap_at, margin + tap_at + half_per * (elems - 1) + 1, half_per, along
        )
        for tap_at in range(tap_count)
    ]
    pieces = []
    for residue in range(period):
        running = None
        for tap_at in range(tap_count):
            if table[residue, tap_at] != 0.0:
                portion = float(table[residue, tap_at]) * columns[tap_at]
                running = portion if running is None else running + portion
        pieces.append(running)
    return alternate(pieces, along)


def prolong_all(field, degree):
    table = PROLONG_TABLES[degree]
    fine = prolong_line(field, 2, table, 1)
    fine = prolong_line(fine, 3, table, 1)
    fine = jnp.pad(fine, [(0, 0)] * 4 + [(1, 1)])
    return prolong_line(fine, 4, table, 1)


def face_pad(field, width):
    return padded_2(field, (("gx", 2), ("gy", 3)), width)


def residual_rims(field, width):
    upper = lax.slice_in_dim(field, field.shape[2] - width, field.shape[2], 1, 2)
    field = jnp.concatenate([passed_along(upper, "gx", 1), field], 2)
    upper = lax.slice_in_dim(field, field.shape[3] - width, field.shape[3], 1, 3)
    return jnp.concatenate([passed_along(upper, "gy", 1), field], 3)


def lift_rims(field):
    first = lax.slice_in_dim(field, 0, 1, 1, 2)
    field = jnp.concatenate([field, passed_along(first, "gx", -1)], 2)
    first = lax.slice_in_dim(field, 0, 1, 1, 3)
    field = jnp.concatenate([field, passed_along(first, "gy", -1)], 3)
    return jnp.pad(field, [(0, 0), (0, 0), (1, 0), (1, 0), (0, 0)])


def restrict_lower(field, degree):
    widths = [(0, 0), (0, 0), (0, degree - 1), (0, degree - 1), (0, 0)]
    return restrict_all(jnp.pad(field, widths), degree - 1, degree)


def line_pad(field, width):
    widths = [(0, 0)] * field.ndim
    widths[-2] = (width, width)
    return padded_2(jnp.pad(field, widths), (("gx", 2),), width)


def coarse_smooth(source, scaling, pinned_f, tables, bounds):
    line_src, line_scale, line_fixed = (
        lax.all_gather(source, "gy", axis=3, tiled=True),
        lax.all_gather(scaling, "gy", axis=1, tiled=True),
        lax.all_gather(pinned_f, "gy", axis=1, tiled=True),
    )
    inverse = inverse_diag(line_scale, line_fixed, tables)[None]
    whole = chebyshev(
        line_src,
        None,
        COARSE_DEG,
        bounds,
        inverse,
        lambda field: operate(field, line_scale, line_fixed, tables, line_pad),
    )
    return lax.dynamic_slice_in_dim(
        whole, lax.axis_index("gy") * source.shape[3], source.shape[3], 3
    )


def local(modes, moduli, pinned, spectrum):
    degrees = [4, 2, 1]
    tables = [basis_tables(degree) for degree in degrees]
    fields = [level_fields(moduli, pinned, stride) for stride in (1, 2, 4)]

    def v_cycle(level_at, source):
        scaling, pinned_f = fields[level_at]
        if level_at == 2:
            return coarse_smooth(source, scaling, pinned_f, tables[2], spectrum[2])
        inverse = inverse_diag(scaling, pinned_f, tables[level_at])[None]

        def apply_op(field):
            return operate(field, scaling, pinned_f, tables[level_at], face_pad)

        degree = degrees[level_at]
        solution = chebyshev(source, None, DEG, spectrum[level_at], inverse, apply_op)
        residual = (1.0 - pinned_f) * source - scaling * elastic(
            face_pad(scaling * solution, degree), tables[level_at], degree
        )
        restricted = restrict_lower(residual_rims(residual, degree - 1), degree)
        coarse_fixed = fields[level_at + 1][1]
        coarse_src = (1.0 - coarse_fixed) * restricted
        lifted = v_cycle(level_at + 1, coarse_src)
        solution = solution + (1.0 - pinned_f) * prolong_all(lift_rims(lifted), degree)
        return chebyshev(source, solution, DEG, spectrum[level_at], inverse, apply_op)

    return v_cycle(0, modes)


def solution(mesh):
    placed = (P(None, None, "gx", "gy", None), P("gx", "gy", None), P("gx", "gy", None), P())
    return jax.shard_map(
        local,
        mesh=mesh,
        in_specs=placed,
        out_specs=P(None, None, "gx", "gy", None),
        check_vma=False,
    )
```

profile of v0, /device:TPU:1, one launch (start us, length us, event | category | flops | bytes accessed | tf_op | source)
XLA Modules:
  0.0 588.4 jit_solution(3534011921018595759)
XLA Ops:
  5.8 4.1 collective-permute-start
  18.2 4.8 collective-permute-start.2
  26.5 4.3 collective-permute-done.3
  41.0 6.4 %multiply_add_fusion.11 = (f32[2,3,20,24,128]{4,3,2,0,1:T(8,128)S(1)}, f32[2,3,20,24,128]{4,3,2,0,1:T(8,128)S(1)}) fusion(f32[2,3,20,24,128]{4,3,2,0,1:T(8,128)S(1)} %copy.3239, f32[128]{0:T(128)S(1)} %copy-done.117, f32[128]{0:T(128)S(1)} %copy-done.121, f32[128]{0:T(128)S(1)} %copy-done.125, f32[128]{0:T(128)S(1)} %copy-done.129, f32[128]{0:T(128)S(1)} %copy-done.133, ...), kind=kLoop, calls=%fused_computation.211 | loop fusion | flops 12533760 | bytes 4431872 | tf_op jit(solution)/shard_map/add | solution.py:126
  54.7 4.2 collective-permute-start.4
  73.3 4.4 collective-permute-done.7
  87.8 6.7 %multiply_add_fusion.9 = (f32[2,3,20,24,128]{4,3,2,0,1:T(8,128)S(1)}, f32[2,3,20,24,128]{4,3,2,0,1:T(8,128)S(1)}) fusion(f32[2,3,20,24,128]{4,3,2,0,1:T(8,128)S(1)} %copy.3247, f32[128]{0:T(128)S(1)} %copy-done.118, f32[128]{0:T(128)S(1)} %copy-done.122, f32[128]{0:T(128)S(1)} %copy-done.126, f32[128]{0:T(128)S(1)} %copy-done.130, f32[128]{0:T(128)S(1)} %copy-done.134, ...), kind=kLoop, calls=%fused_computation.209 | loop fusion | flops 12533760 | bytes 4431872 | tf_op jit(solution)/shard_map/add | solution.py:126
  104.1 4.5 collective-permute-start.8
  109.9 5.5 collective-permute-done.8
  135.2 6.5 %multiply_add_fusion.7 = (f32[2,3,20,24,128]{4,3,2,0,1:T(8,128)S(1)}, f32[2,3,20,24,128]{4,3,2,0,1:T(8,128)S(1)}) fusion(f32[2,3,20,24,128]{4,3,2,0,1:T(8,128)S(1)} %copy.3256, f32[128]{0:T(128)S(1)} %copy-done.119, f32[128]{0:T(128)S(1)} %copy-done.123, f32[128]{0:T(128)S(1)} %copy-done.127, f32[128]{0:T(128)S(1)} %copy-done.131, f32[128]{0:T(128)S(1)} %copy-done.135, ...), kind=kLoop, calls=%fused_computation.207 | loop fusion | flops 12533760 | bytes 4431872 | tf_op jit(solution)/shard_map/add | solution.py:126
  175.1 4.1 collective-permute-start.14
  180.5 4.4 collective-permute-done.15
  185.0 5.5 collective-permute-start.16
  206.0 4.5 collective-permute-start.18
  251.6 4.4 all_gather.10
  256.0 5.2 all_gather.9
  276.1 4.3 collective-permute-start.26
  286.9 6.2 %all_gather.11 = f32[2,3,3,16,32]{4,0,2,1,3:T(2,128)S(1)} all-gather(f32[2,3,3,4,32]{4,0,2,1,3:T(2,128)S(1)} %copy.3320), channel_id=1, replica_groups=mesh['gx'=8,'gy'=4] {'gy'}, dimensions={3}, use_global_device_ids=true | all-gather | bytes 46080 | tf_op jit(solution)/shard_map/all_gather | solution.py:325
  329.9 7.0 %collective-permute-start.35 = (f32[2,3,4,1,32]{4,3,2,1,0:T(1,128)S(1)}, f32[2,3,4,1,32]{4,3,2,1,0:T(1,128)S(1)}, u32[]{:S(2)}, u32[]{:S(2)}) collective-permute-start(f32[2,3,4,1,32]{4,3,2,1,0:T(1,128)S(1)} %fusion.1578), channel_id=1, source_target_pairs={{1,0},{2,1},{3,2},{5,4},{6,5},{7,6},{9,8},{10,9},{11,10},{13,12},{... | collective-permute-start | bytes 9224 | tf_op jit(solution)/shard_map/ppermute | solution.py:62
  432.5 5.4 slice.8786
  438.0 5.4 slice.8785
  443.4 5.4 slice.8787
  462.0 6.0 %collective-permute-done.50 = f32[2,3,4,16,128]{4,3,2,1,0:T(8,128)S(1)} collective-permute-done((f32[2,3,4,16,128]{4,3,2,1,0:T(8,128)S(1)}, f32[2,3,4,16,128]{4,3,2,1,0:T(8,128)S(1)}, u32[]{:S(2)}, u32[]{:S(2)}) %collective-permute-start.50) | collective-permute-done | bytes 196640 | tf_op jit(solution)/shard_map/ppermute | solution.py:50
  473.9 4.8 collective-permute-done.53
  487.0 6.7 %multiply_add_fusion.5 = (f32[2,3,20,24,128]{4,3,2,0,1:T(8,128)S(1)}, f32[2,3,20,24,128]{4,3,2,0,1:T(8,128)S(1)}) fusion(f32[2,3,20,24,128]{4,3,2,0,1:T(8,128)S(1)} %copy.3374, f32[128]{0:T(128)S(1)} %copy-done.120, f32[128]{0:T(128)S(1)} %copy-done.124, f32[128]{0:T(128)S(1)} %copy-done.128, f32[128]{0:T(128)S(1)} %copy-done.132, f32[128]{0:T(128)S(1)} %copy-done.136, ...), kind=kLoop, calls=%fused_computation.205 | loop fusion | flops 12533760 | bytes 4431872 | tf_op jit(solution)/shard_map/add | solution.py:126
  502.4 4.1 collective-permute-start.54
  507.9 5.5 collective-permute-done.54
  519.4 4.4 collective-permute-done.57
  530.4 6.3 %multiply_add_fusion.3 = (f32[2,3,20,24,128]{4,3,2,0,1:T(8,128)S(1)}, f32[2,3,20,24,128]{4,3,2,0,1:T(8,128)S(1)}) fusion(f32[2,3,20,24,128]{4,3,2,0,1:T(8,128)S(1)} %copy.3383, f32[128]{0:T(128)S(1)} %copy-done.120, f32[128]{0:T(128)S(1)} %copy-done.124, f32[128]{0:T(128)S(1)} %copy-done.128, f32[128]{0:T(128)S(1)} %copy-done.132, f32[128]{0:T(128)S(1)} %copy-done.136, ...), kind=kLoop, calls=%fused_computation.203 | loop fusion | flops 12533760 | bytes 4431872 | tf_op jit(solution)/shard_map/add | solution.py:126
  549.8 5.0 collective-permute-done.58
  561.3 4.4 collective-permute-done.61
  572.3 6.5 %multiply_add_fusion.1 = (f32[2,3,20,24,128]{4,3,2,0,1:T(8,128)S(1)}, f32[2,3,20,24,128]{4,3,2,0,1:T(8,128)S(1)}) fusion(f32[2,3,20,24,128]{4,3,2,0,1:T(8,128)S(1)} %copy.3392, f32[128]{0:T(128)S(1)} %copy-done.120, f32[128]{0:T(128)S(1)} %copy-done.124, f32[128]{0:T(128)S(1)} %copy-done.128, f32[128]{0:T(128)S(1)} %copy-done.132, f32[128]{0:T(128)S(1)} %copy-done.136, ...), kind=kLoop, calls=%fused_computation.201 | loop fusion | flops 12533760 | bytes 4431872 | tf_op jit(solution)/shard_map/add | solution.py:126
  (1334 shorter events, 404.8 us)
Async XLA Ops:
  5.8 7.7 %collective-permute-start = (f32[2,3,4,16,128]{4,3,2,1,0:T(8,128)S(1)}, f32[2,3,4,16,128]{4,3,2,1,0:T(8,128)S(1)}, u32[]{:S(2)}, u32[]{:S(2)}) collective-permute-start(f32[2,3,4,16,128]{4,3,2,1,0:T(8,128)S(1)} %get-tuple-element.87), channel_id=1, source_target_pairs={{0,4},{4,8},{8,12},{12,16},{16,20},{20,24},{24,28},{1,5},{5,9},{9,... | collective-permute-start | bytes 589832 | tf_op jit(solution)/shard_map/ppermute | solution.py:50
  9.9 7.4 %collective-permute-start.1 = (f32[2,3,4,16,128]{4,3,2,1,0:T(8,128)S(1)}, f32[2,3,4,16,128]{4,3,2,1,0:T(8,128)S(1)}, u32[]{:S(2)}, u32[]{:S(2)}) collective-permute-start(f32[2,3,4,16,128]{4,3,2,1,0:T(8,128)S(1)} %get-tuple-element.88), channel_id=1, source_target_pairs={{4,0},{8,4},{12,8},{16,12},{20,16},{24,20},{28,24},{5,1},{9,5},{13... | collective-permute-start | bytes 589832 | tf_op jit(solution)/shard_map/ppermute | solution.py:52
  18.2 8.2 %collective-permute-start.2 = (f32[2,3,20,4,128]{4,3,2,1,0:T(4,128)}, f32[2,3,20,4,128]{4,3,2,1,0:T(4,128)S(1)}, u32[]{:S(2)}, u32[]{:S(2)}) collective-permute-start(f32[2,3,20,4,128]{4,3,2,1,0:T(4,128)} %get-tuple-element.73), channel_id=1, source_target_pairs={{0,1},{1,2},{2,3},{4,5},{5,6},{6,7},{8,9},{9,10},{10,11},{12,13},{... | collective-permute-start | bytes 737288 | tf_op jit(solution)/shard_map/ppermute | solution.py:50
  23.0 7.7 %collective-permute-start.3 = (f32[2,3,20,4,128]{4,3,2,1,0:T(4,128)}, f32[2,3,20,4,128]{4,3,2,1,0:T(4,128)S(1)}, u32[]{:S(2)}, u32[]{:S(2)}) collective-permute-start(f32[2,3,20,4,128]{4,3,2,1,0:T(4,128)} %get-tuple-element.74), channel_id=1, source_target_pairs={{1,0},{2,1},{3,2},{5,4},{6,5},{7,6},{9,8},{10,9},{11,10},{13,12},{... | collective-permute-start | bytes 737288 | tf_op jit(solution)/shard_map/ppermute | solution.py:52
  54.7 8.9 %collective-permute-start.4 = (f32[2,3,4,16,128]{4,3,2,1,0:T(8,128)S(1)}, f32[2,3,4,16,128]{4,3,2,1,0:T(8,128)S(1)}, u32[]{:S(2)}, u32[]{:S(2)}) collective-permute-start(f32[2,3,4,16,128]{4,3,2,1,0:T(8,128)S(1)} %get-tuple-element.85), channel_id=1, source_target_pairs={{0,4},{4,8},{8,12},{12,16},{16,20},{20,24},{24,28},{1,5},{5,9},{9,... | collective-permute-start | bytes 589832 | tf_op jit(solution)/shard_map/ppermute | solution.py:50
  58.9 7.1 %collective-permute-start.5 = (f32[2,3,4,16,128]{4,3,2,1,0:T(8,128)S(1)}, f32[2,3,4,16,128]{4,3,2,1,0:T(8,128)S(1)}, u32[]{:S(2)}, u32[]{:S(2)}) collective-permute-start(f32[2,3,4,16,128]{4,3,2,1,0:T(8,128)S(1)} %get-tuple-element.86), channel_id=1, source_target_pairs={{4,0},{8,4},{12,8},{16,12},{20,16},{24,20},{28,24},{5,1},{9,5},{13... | collective-permute-start | bytes 589832 | tf_op jit(solution)/shard_map/ppermute | solution.py:52
  66.9 6.4 %collective-permute-start.6 = (f32[2,3,20,4,128]{4,3,2,1,0:T(4,128)}, f32[2,3,20,4,128]{4,3,2,1,0:T(4,128)}, u32[]{:S(2)}, u32[]{:S(2)}) collective-permute-start(f32[2,3,20,4,128]{4,3,2,1,0:T(4,128)} %get-tuple-element.71), channel_id=1, source_target_pairs={{0,1},{1,2},{2,3},{4,5},{5,6},{6,7},{8,9},{9,10},{10,11},{12,13},{... | collective-permute-start | bytes 737288 | tf_op jit(solution)/shard_map/ppermute | solution.py:50
  69.9 7.8 %collective-permute-start.7 = (f32[2,3,20,4,128]{4,3,2,1,0:T(4,128)}, f32[2,3,20,4,128]{4,3,2,1,0:T(4,128)}, u32[]{:S(2)}, u32[]{:S(2)}) collective-permute-start(f32[2,3,20,4,128]{4,3,2,1,0:T(4,128)} %get-tuple-element.72), channel_id=1, source_target_pairs={{1,0},{2,1},{3,2},{5,4},{6,5},{7,6},{9,8},{10,9},{11,10},{13,12},{... | collective-permute-start | bytes 737288 | tf_op jit(solution)/shard_map/ppermute | solution.py:52
  104.1 11.4 %collective-permute-start.8 = (f32[2,3,4,16,128]{4,3,2,1,0:T(8,128)S(1)}, f32[2,3,4,16,128]{4,3,2,1,0:T(8,128)S(1)}, u32[]{:S(2)}, u32[]{:S(2)}) collective-permute-start(f32[2,3,4,16,128]{4,3,2,1,0:T(8,128)S(1)} %get-tuple-element.83), channel_id=1, source_target_pairs={{0,4},{4,8},{8,12},{12,16},{16,20},{20,24},{24,28},{1,5},{5,9},{9,... | collective-permute-start | bytes 589832 | tf_op jit(solution)/shard_map/ppermute | solution.py:50
  108.6 6.8 %collective-permute-start.9 = (f32[2,3,4,16,128]{4,3,2,1,0:T(8,128)S(1)}, f32[2,3,4,16,128]{4,3,2,1,0:T(8,128)S(1)}, u32[]{:S(2)}, u32[]{:S(2)}) collective-permute-start(f32[2,3,4,16,128]{4,3,2,1,0:T(8,128)S(1)} %get-tuple-element.84), channel_id=1, source_target_pairs={{4,0},{8,4},{12,8},{16,12},{20,16},{24,20},{28,24},{5,1},{9,5},{13... | collective-permute-start | bytes 589832 | tf_op jit(solution)/shard_map/ppermute | solution.py:52
  115.5 11.5 %collective-permute-start.10 = (f32[2,3,20,4,128]{4,3,2,1,0:T(4,128)S(1)}, f32[2,3,20,4,128]{4,3,2,1,0:T(4,128)S(1)}, u32[]{:S(2)}, u32[]{:S(2)}) collective-permute-start(f32[2,3,20,4,128]{4,3,2,1,0:T(4,128)S(1)} %get-tuple-element.69), channel_id=1, source_target_pairs={{0,1},{1,2},{2,3},{4,5},{5,6},{6,7},{8,9},{9,10},{10,11},{12,13},{... | collective-permute-start | bytes 737288 | tf_op jit(solution)/shard_map/ppermute | solution.py:50
  118.3 8.7 %collective-permute-start.11 = (f32[2,3,20,4,128]{4,3,2,1,0:T(4,128)S(1)}, f32[2,3,20,4,128]{4,3,2,1,0:T(4,128)S(1)}, u32[]{:S(2)}, u32[]{:S(2)}) collective-permute-start(f32[2,3,20,4,128]{4,3,2,1,0:T(4,128)S(1)} %get-tuple-element.70), channel_id=1, source_target_pairs={{1,0},{2,1},{3,2},{5,4},{6,5},{7,6},{9,8},{10,9},{11,10},{13,12},{... | collective-permute-start | bytes 737288 | tf_op jit(solution)/shard_map/ppermute | solution.py:52
  150.2 7.0 %collective-permute-start.12 = (f32[2,3,3,16,128]{4,3,2,1,0:T(8,128)S(1)}, f32[2,3,3,16,128]{4,3,2,1,0:T(8,128)S(1)}, u32[]{:S(2)}, u32[]{:S(2)}) collective-permute-start(f32[2,3,3,16,128]{4,3,2,1,0:T(8,128)S(1)} %slice.9865), channel_id=1, source_target_pairs={{0,4},{4,8},{8,12},{12,16},{16,20},{20,24},{24,28},{1,5},{5,9},{9,... | collective-permute-start | bytes 442376 | tf_op jit(solution)/shard_map/ppermute | solution.py:62
  179.2 5.7 collective-permute-start.15
  185.0 7.5 %collective-permute-start.16 = (f32[2,3,10,2,64]{4,3,2,1,0:T(2,128)S(1)}, f32[2,3,10,2,64]{4,3,2,1,0:T(2,128)S(1)}, u32[]{:S(2)}, u32[]{:S(2)}) collective-permute-start(f32[2,3,10,2,64]{4,3,2,1,0:T(2,128)S(1)} %get-tuple-element.183), channel_id=1, source_target_pairs={{0,1},{1,2},{2,3},{4,5},{5,6},{6,7},{8,9},{9,10},{10,11},{12,13},{... | collective-permute-start | bytes 92168 | tf_op jit(solution)/shard_map/ppermute | solution.py:50
  206.0 5.8 collective-permute-start.18
  215.4 8.9 %collective-permute-start.20 = (f32[2,3,10,2,64]{4,3,2,1,0:T(2,128)S(1)}, f32[2,3,10,2,64]{4,3,2,1,0:T(2,128)S(1)}, u32[]{:S(2)}, u32[]{:S(2)}) collective-permute-start(f32[2,3,10,2,64]{4,3,2,1,0:T(2,128)S(1)} %get-tuple-element.181), channel_id=1, source_target_pairs={{0,1},{1,2},{2,3},{4,5},{5,6},{6,7},{8,9},{9,10},{10,11},{12,13},{... | collective-permute-start | bytes 92168 | tf_op jit(solution)/shard_map/ppermute | solution.py:50
  245.9 17.6 %collective-permute-start.24 = (f32[2,3,10,2,64]{4,3,2,1,0:T(2,128)S(1)}, f32[2,3,10,2,64]{4,3,2,1,0:T(2,128)S(1)}, u32[]{:S(2)}, u32[]{:S(2)}) collective-permute-start(f32[2,3,10,2,64]{4,3,2,1,0:T(2,128)S(1)} %get-tuple-element.179), channel_id=1, source_target_pairs={{0,1},{1,2},{2,3},{4,5},{5,6},{6,7},{8,9},{9,10},{10,11},{12,13},{... | collective-permute-start | bytes 92168 | tf_op jit(solution)/shard_map/ppermute | solution.py:50
  293.1 6.3 %collective-permute-start.28 = (f32[2,3,1,18,32]{4,3,2,0,1:T(8,128)S(1)}, f32[2,3,1,18,32]{4,3,2,0,1:T(8,128)S(1)}, u32[]{:S(2)}, u32[]{:S(2)}) collective-permute-start(f32[2,3,1,18,32]{4,3,2,0,1:T(8,128)S(1)} %get-tuple-element.200), channel_id=1, source_target_pairs={{0,4},{4,8},{8,12},{12,16},{16,20},{20,24},{24,28},{1,5},{5,9},{9,... | collective-permute-start | bytes 41480 | tf_op jit(solution)/shard_map/ppermute | solution.py:50
  329.9 9.8 %collective-permute-start.35 = (f32[2,3,4,1,32]{4,3,2,1,0:T(1,128)S(1)}, f32[2,3,4,1,32]{4,3,2,1,0:T(1,128)S(1)}, u32[]{:S(2)}, u32[]{:S(2)}) collective-permute-start(f32[2,3,4,1,32]{4,3,2,1,0:T(1,128)S(1)} %fusion.1578), channel_id=1, source_target_pairs={{1,0},{2,1},{3,2},{5,4},{6,5},{7,6},{9,8},{10,9},{11,10},{13,12},{... | collective-permute-start | bytes 9224 | tf_op jit(solution)/shard_map/ppermute | solution.py:62
  457.3 10.8 %collective-permute-start.50 = (f32[2,3,4,16,128]{4,3,2,1,0:T(8,128)S(1)}, f32[2,3,4,16,128]{4,3,2,1,0:T(8,128)S(1)}, u32[]{:S(2)}, u32[]{:S(2)}) collective-permute-start(f32[2,3,4,16,128]{4,3,2,1,0:T(8,128)S(1)} %get-tuple-element.81), channel_id=1, source_target_pairs={{0,4},{4,8},{8,12},{12,16},{16,20},{20,24},{24,28},{1,5},{5,9},{9,... | collective-permute-start | bytes 589832 | tf_op jit(solution)/shard_map/ppermute | solution.py:50
  460.7 7.4 %collective-permute-start.51 = (f32[2,3,4,16,128]{4,3,2,1,0:T(8,128)S(1)}, f32[2,3,4,16,128]{4,3,2,1,0:T(8,128)S(1)}, u32[]{:S(2)}, u32[]{:S(2)}) collective-permute-start(f32[2,3,4,16,128]{4,3,2,1,0:T(8,128)S(1)} %get-tuple-element.82), channel_id=1, source_target_pairs={{4,0},{8,4},{12,8},{16,12},{20,16},{24,20},{28,24},{5,1},{9,5},{13... | collective-permute-start | bytes 589832 | tf_op jit(solution)/shard_map/ppermute | solution.py:52
  468.2 5.7 collective-permute-start.52
  471.0 7.6 %collective-permute-start.53 = (f32[2,3,20,4,128]{4,3,2,1,0:T(4,128)S(1)}, f32[2,3,20,4,128]{4,3,2,1,0:T(4,128)S(1)}, u32[]{:S(2)}, u32[]{:S(2)}) collective-permute-start(f32[2,3,20,4,128]{4,3,2,1,0:T(4,128)S(1)} %get-tuple-element.68), channel_id=1, source_target_pairs={{1,0},{2,1},{3,2},{5,4},{6,5},{7,6},{9,8},{10,9},{11,10},{13,12},{... | collective-permute-start | bytes 737288 | tf_op jit(solution)/shard_map/ppermute | solution.py:52
  502.4 10.9 %collective-permute-start.54 = (f32[2,3,4,16,128]{4,3,2,1,0:T(8,128)S(1)}, f32[2,3,4,16,128]{4,3,2,1,0:T(8,128)S(1)}, u32[]{:S(2)}, u32[]{:S(2)}) collective-permute-start(f32[2,3,4,16,128]{4,3,2,1,0:T(8,128)S(1)} %get-tuple-element.79), channel_id=1, source_target_pairs={{0,4},{4,8},{8,12},{12,16},{16,20},{20,24},{24,28},{1,5},{5,9},{9,... | collective-permute-start | bytes 589832 | tf_op jit(solution)/shard_map/ppermute | solution.py:50
  506.6 6.8 %collective-permute-start.55 = (f32[2,3,4,16,128]{4,3,2,1,0:T(8,128)S(1)}, f32[2,3,4,16,128]{4,3,2,1,0:T(8,128)S(1)}, u32[]{:S(2)}, u32[]{:S(2)}) collective-permute-start(f32[2,3,4,16,128]{4,3,2,1,0:T(8,128)S(1)} %get-tuple-element.80), channel_id=1, source_target_pairs={{4,0},{8,4},{12,8},{16,12},{20,16},{24,20},{28,24},{5,1},{9,5},{13... | collective-permute-start | bytes 589832 | tf_op jit(solution)/shard_map/ppermute | solution.py:52
  513.4 5.9 %collective-permute-start.56 = (f32[2,3,20,4,128]{4,3,2,1,0:T(4,128)S(1)}, f32[2,3,20,4,128]{4,3,2,1,0:T(4,128)S(1)}, u32[]{:S(2)}, u32[]{:S(2)}) collective-permute-start(f32[2,3,20,4,128]{4,3,2,1,0:T(4,128)S(1)} %get-tuple-element.65), channel_id=1, source_target_pairs={{0,1},{1,2},{2,3},{4,5},{5,6},{6,7},{8,9},{9,10},{10,11},{12,13},{... | collective-permute-start | bytes 737288 | tf_op jit(solution)/shard_map/ppermute | solution.py:50
  516.2 7.5 %collective-permute-start.57 = (f32[2,3,20,4,128]{4,3,2,1,0:T(4,128)S(1)}, f32[2,3,20,4,128]{4,3,2,1,0:T(4,128)S(1)}, u32[]{:S(2)}, u32[]{:S(2)}) collective-permute-start(f32[2,3,20,4,128]{4,3,2,1,0:T(4,128)S(1)} %get-tuple-element.66), channel_id=1, source_target_pairs={{1,0},{2,1},{3,2},{5,4},{6,5},{7,6},{9,8},{10,9},{11,10},{13,12},{... | collective-permute-start | bytes 737288 | tf_op jit(solution)/shard_map/ppermute | solution.py:52
  544.8 10.0 %collective-permute-start.58 = (f32[2,3,4,16,128]{4,3,2,1,0:T(8,128)S(1)}, f32[2,3,4,16,128]{4,3,2,1,0:T(8,128)S(1)}, u32[]{:S(2)}, u32[]{:S(2)}) collective-permute-start(f32[2,3,4,16,128]{4,3,2,1,0:T(8,128)S(1)} %get-tuple-element.77), channel_id=1, source_target_pairs={{0,4},{4,8},{8,12},{12,16},{16,20},{20,24},{24,28},{1,5},{5,9},{9,... | collective-permute-start | bytes 589832 | tf_op jit(solution)/shard_map/ppermute | solution.py:50
  548.5 6.4 %collective-permute-start.59 = (f32[2,3,4,16,128]{4,3,2,1,0:T(8,128)S(1)}, f32[2,3,4,16,128]{4,3,2,1,0:T(8,128)S(1)}, u32[]{:S(2)}, u32[]{:S(2)}) collective-permute-start(f32[2,3,4,16,128]{4,3,2,1,0:T(8,128)S(1)} %get-tuple-element.78), channel_id=1, source_target_pairs={{4,0},{8,4},{12,8},{16,12},{20,16},{24,20},{28,24},{5,1},{9,5},{13... | collective-permute-start | bytes 589832 | tf_op jit(solution)/shard_map/ppermute | solution.py:52
  555.0 6.3 %collective-permute-start.60 = (f32[2,3,20,4,128]{4,3,2,1,0:T(4,128)S(1)}, f32[2,3,20,4,128]{4,3,2,1,0:T(4,128)S(1)}, u32[]{:S(2)}, u32[]{:S(2)}) collective-permute-start(f32[2,3,20,4,128]{4,3,2,1,0:T(4,128)S(1)} %get-tuple-element.63), channel_id=1, source_target_pairs={{0,1},{1,2},{2,3},{4,5},{5,6},{6,7},{8,9},{9,10},{10,11},{12,13},{... | collective-permute-start | bytes 737288 | tf_op jit(solution)/shard_map/ppermute | solution.py:50
  558.2 7.5 %collective-permute-start.61 = (f32[2,3,20,4,128]{4,3,2,1,0:T(4,128)S(1)}, f32[2,3,20,4,128]{4,3,2,1,0:T(4,128)S(1)}, u32[]{:S(2)}, u32[]{:S(2)}) collective-permute-start(f32[2,3,20,4,128]{4,3,2,1,0:T(4,128)S(1)} %get-tuple-element.64), channel_id=1, source_target_pairs={{1,0},{2,1},{3,2},{5,4},{6,5},{7,6},{9,8},{10,9},{11,10},{13,12},{... | collective-permute-start | bytes 737288 | tf_op jit(solution)/shard_map/ppermute | solution.py:52
  (416 other events, 1669.6 us)
where the time goes:
time: 598 us; the launch traced here: 588 us
  other arithmetic  199 us (33%)
  starting transfers between devices  166 us (28%)
  waiting for transfers between devices  130 us (22%)
  local copies, waits for them, and re-layouts  61.8 us (10%)
  between operations  16.4 us (3%)
  blocking collectives  15.7 us (3%)
    add x186, other arithmetic, line_apply(): summed = weighted if summed is None else summed + weighted  166 us
    ppermute x27, starting transfers between devices, padded_2(): lax.ppermute(tail, axis, [(i, (i + 1) % count) for i in range(ends)])  96 us
    ppermute x27, waiting for transfers between devices, padded_2(): lax.ppermute(head, axis, [((i + 1) % count, i) for i in range(ends)])  79.5 us
    ppermute x27, starting transfers between devices, padded_2(): lax.ppermute(head, axis, [((i + 1) % count, i) for i in range(ends)])  45 us
    ppermute x27, waiting for transfers between devices, padded_2(): lax.ppermute(tail, axis, [(i, (i + 1) % count) for i in range(ends)])  33 us
    ppermute x8, starting transfers between devices, passed_along(): return lax.ppermute(value, axis, pairs)  24.7 us
    unnamed x792, local copies, waits for them, and re-layouts  19.4 us
    ppermute x8, waiting for transfers between devices, passed_along(): return lax.ppermute(value, axis, pairs)  17.5 us
  transfers between devices with their start and end apart: 62, of which 42 were waited for; matrix products, arithmetic and copies ran while one was open for 2% of the time, Pallas kernels for 0%

commit v1 on v0

v1 whole, which is shorter than its diff:
```python
import functools

import jax
import jax.numpy as jnp
import numpy as np
from jax import lax
from jax.experimental import pallas as pl
from jax.experimental.pallas import tpu as pltpu
from jax.sharding import PartitionSpec as P

DEG = 3
COARSE_DEG = 4
DEGREES = (4, 2, 1)
MU_SHEAR = 1.0
LAMBDA_BULK = 1.5
PROLONG_TABLES = {
    4: np.array(
        [[1.0, 0.0, 0.0], [0.375, 0.75, -0.125], [0.0, 1.0, 0.0], [-0.125, 0.75, 0.375]]
    ),
    2: np.array([[1.0, 0.0], [0.5, 0.5]]),
}
DIRS = ((-1, 0), (0, -1), (1, 0), (0, 1), (-1, -1), (-1, 1), (1, -1), (1, 1))
F32 = jnp.float32
BF16 = jnp.bfloat16


def assemble(element, degree):
    table = np.zeros((degree, 2 * degree + 1))
    for residue in range(degree):
        for offset in range(-degree, degree + 1):
            target = residue + offset
            if 0 <= target <= degree:
                table[residue, offset + degree] += element[residue, target]
            if residue == 0 and offset <= 0:
                table[residue, offset + degree] += element[degree, degree + offset]
    return table


def basis_tables(degree):
    nodes = [float(place) / degree for place in range(degree + 1)]
    gauss_x, gauss_w = np.polynomial.legendre.leggauss(8)
    points = 0.5 * (gauss_x + 1.0)
    weights = 0.5 * gauss_w
    values = np.zeros((degree + 1, points.size))
    slopes = np.zeros((degree + 1, points.size))
    for column in range(degree + 1):
        product = np.ones(points.size)
        for other in range(degree + 1):
            if other != column:
                product = product * (points - nodes[other]) / (nodes[column] - nodes[other])
        values[column] = product
        for skipped in range(degree + 1):
            if skipped != column:
                part = np.ones(points.size) / (nodes[column] - nodes[skipped])
                for other in range(degree + 1):
                    if other != column and other != skipped:
                        part = part * (points - nodes[other]) / (nodes[column] - nodes[other])
                slopes[column] += part
    mass = (values * weights) @ values.T
    stiff = (slopes * weights) @ slopes.T
    mixed = (slopes * weights) @ values.T
    return [assemble(e, degree) for e in (mass, stiff, mixed, mixed.T)]


def dense(table, count):
    p = table.shape[0]
    out = np.zeros((count, count + p + 1))
    for i in range(count):
        for o in range(-p, p + 1):
            c = table[i % p, o + p]
            if c != 0.0 and i + o <= count:
                out[i, i + o + p] += c
    return out


def up8(n):
    return -(-n // 8) * 8


class Level:
    def __init__(self, degree, nx, ny, nz, vecs):
        p = self.p = degree
        self.nx, self.ny, self.nz, self.vecs = nx, ny, nz, vecs
        self.own = nx * ny
        self.rows = up8(self.own)
        self.lanes = -(-vecs * nz // 128) * 128
        self.pos = [(x, y) for x in range(nx) for y in range(ny)]
        self.pos += [None] * (self.rows - self.own)
        self.blocks = []
        self.halo_pos = []
        for dx, dy in DIRS:
            src_x = {-1: range(nx - p, nx), 0: range(nx), 1: range(1)}[dx]
            src_y = {-1: range(ny - p, ny), 0: range(ny), 1: range(1)}[dy]
            start = len(self.halo_pos)
            runs = []
            for x in src_x:
                at = len(self.halo_pos)
                runs.append((at, x * ny + src_y[0], len(src_y)))
                self.halo_pos += [(x + dx * nx, y + dy * ny) for y in src_y]
            merged = [runs[0]]
            for run in runs[1:]:
                a, b, n = merged[-1]
                if run[0] == a + n and run[1] == b + n:
                    merged[-1] = (a, b, n + run[2])
                else:
                    merged.append(run)
            size = up8(len(self.halo_pos) - start)
            self.halo_pos += [None] * (start + size - len(self.halo_pos))
            self.blocks.append((start, size, merged))
        self.halo = len(self.halo_pos)

    def plane(self, mat_x, mat_y, rows_out, positions):
        out = np.zeros((rows_out, len(positions)))
        for k, at in enumerate(positions):
            if at is not None:
                col = np.outer(mat_x[:, at[0] + self.p], mat_y[:, at[1] + self.p]).ravel()
                out[: col.size, k] = col
        return out

    def operator(self):
        t = basis_tables(self.p)
        m_x, k_x, g_x, t_x = [dense(e, self.nx) for e in t]
        m_y, k_y, g_y, t_y = [dense(e, self.ny) for e in t]
        cc = LAMBDA_BULK + MU_SHEAR
        big = MU_SHEAR + cc
        groups = [
            [((big, k_x, m_y), (MU_SHEAR, m_x, k_y)), ((1, m_x, m_y),), ((cc, t_x, g_y),), ((cc, t_x, m_y),)],
            [((MU_SHEAR, k_x, m_y), (big, m_x, k_y)), ((1, m_x, m_y),), ((cc, g_x, t_y),), ((cc, m_x, t_y),)],
            [((MU_SHEAR, k_x, m_y), (MU_SHEAR, m_x, k_y)), ((1, m_x, m_y),), ((cc, g_x, m_y),), ((cc, m_x, g_y),)],
        ]

        def build(positions):
            return np.stack(
                [
                    np.concatenate(
                        [
                            sum(w * self.plane(a, b, self.rows, positions) for w, a, b in terms)
                            for terms in source
                        ]
                    )
                    for source in groups
                ]
            )

        line = [self.lift_z(dense(e, self.nz)[:, self.p : self.p + self.nz], self) for e in t]
        z_ops = np.stack([line[0], MU_SHEAR * line[1], big * line[1], line[2], line[3]])
        return build(self.pos), build(self.halo_pos), z_ops

    def lift_z(self, mat, to):
        full = np.kron(np.eye(self.vecs), mat.T)
        out = np.zeros((self.lanes, to.lanes))
        out[: full.shape[0], : full.shape[1]] = full
        return out

    def diagonal(self):
        t = basis_tables(self.p)

        def center(table, count):
            return table[np.arange(count) % self.p, self.p]

        m = [center(t[0], n) for n in (self.nx, self.ny, self.nz)]
        k = [center(t[1], n) for n in (self.nx, self.ny, self.nz)]
        out = np.zeros((3, self.nx, self.ny, self.nz))
        for c in range(3):
            for e in range(3):
                coef = MU_SHEAR + (LAMBDA_BULK + MU_SHEAR) * (c == e)
                f = [k[i] if i == e else m[i] for i in range(3)]
                out[c] += coef * f[0][:, None, None] * f[1][None, :, None] * f[2][None, None, :]
        return out.astype(np.float32)


def prolong_dense(table, fine_n, lead):
    q = table.shape[0]
    half = q // 2
    out = np.zeros((fine_n, fine_n // 2 + lead + 1))
    for i in range(fine_n):
        for t in range(half + 1):
            j = half * (i // q) + t
            out[i, j + lead] += table[i % q, t]
    return out


def restrict_dense(table, fine_n):
    q = table.shape[0]
    half = q // 2
    out = np.zeros((fine_n // 2, fine_n + q + 1))
    for j in range(fine_n // 2):
        for i in range(-q, fine_n):
            t = j - half * (i // q)
            if 0 <= t <= half:
                out[j, i + q] += table[i % q, t]
    return out


def transfer(fine, coarse):
    table = PROLONG_TABLES[fine.p]
    rx, ry = restrict_dense(table, fine.nx), restrict_dense(table, fine.ny)
    rz = restrict_dense(table, fine.nz)[:, fine.p : fine.p + fine.nz]
    px = prolong_dense(table, fine.nx, coarse.p)
    py = prolong_dense(table, fine.ny, coarse.p)
    pz = prolong_dense(table, fine.nz, coarse.p)[:, coarse.p : coarse.p + coarse.nz]
    return (
        fine.plane(rx, ry, coarse.rows, fine.pos),
        fine.plane(rx, ry, coarse.rows, fine.halo_pos),
        fine.lift_z(rz, coarse),
        coarse.plane(px, py, fine.rows, coarse.pos),
        coarse.plane(px, py, fine.rows, coarse.halo_pos),
        coarse.lift_z(pz, fine),
    )


def split(mat):
    mat = np.asarray(mat, np.float32)
    hi = mat.astype(BF16)
    return [hi, (mat - hi.astype(np.float32)).astype(BF16)]


def halves(value):
    hi = value.astype(BF16)
    return hi, (value - hi.astype(F32)).astype(BF16)


def dot3(a, b):
    def one(u, v):
        return lax.dot_general(u, v, (((1,), (0,)), ((), ())), preferred_element_type=F32)

    return one(a[0], b[0]) + one(a[0], b[1]) + one(a[1], b[0])


def kernel(levels, names, *refs):
    R = dict(zip(names, refs))
    gx_n, gy_n = lax.axis_size("gx"), lax.axis_size("gy")
    me_x, me_y = lax.axis_index("gx"), lax.axis_index("gy")

    def reach(dx, dy):
        ok = None
        for d, me, n in ((dx, me_x, gx_n), (dy, me_y, gy_n)):
            if d:
                here = me + d < n if d > 0 else me + d >= 0
                ok = here if ok is None else jnp.logical_and(ok, here)
        return ok

    def device(dx, dy):
        return (jnp.clip(me_x + dx, 0, gx_n - 1), jnp.clip(me_y + dy, 0, gy_n - 1))

    for l, lev in enumerate(levels):
        R[f"halo{l}"][...] = jnp.zeros_like(R[f"halo{l}"])
        R[f"send{l}"][...] = jnp.zeros_like(R[f"send{l}"])
    barrier = pltpu.get_barrier_semaphore()
    for dx, dy in DIRS:

        @pl.when(reach(dx, dy))
        def _():
            pl.semaphore_signal(
                barrier, inc=1, device_id=device(dx, dy), device_id_type=pl.DeviceIdType.MESH
            )

    around = [
        1 + (me > 0).astype(jnp.int32) + (me < n - 1).astype(jnp.int32)
        for me, n in ((me_x, gx_n), (me_y, gy_n))
    ]
    pl.semaphore_wait(barrier, around[0] * around[1] - 1)

    def copies(l, slot):
        for i, (dx, dy) in enumerate(DIRS):
            start, size, _ = levels[l].blocks[i]
            yield (
                dx,
                dy,
                pltpu.make_async_remote_copy(
                    src_ref=R[f"send{l}"].at[:, pl.ds(start, size), :],
                    dst_ref=R[f"halo{l}"].at[slot, :, pl.ds(start, size), :],
                    send_sem=R[f"ssem{l}"].at[i],
                    recv_sem=R[f"rsem{l}"].at[slot, i],
                    device_id=device(-dx, -dy),
                    device_id_type=pl.DeviceIdType.MESH,
                ),
            )

    def exchange(l, slot, value):
        lev = levels[l]
        work, send = R[f"work{l}"], R[f"send{l}"]

        def stage(c, _):
            work[c] = value(c)
            for _, _, runs in lev.blocks:
                for at, src, n in runs:
                    send[c, at : at + n, :] = work[c, src : src + n, :]
            return 0

        lax.fori_loop(0, 3, stage, 0)
        for dx, dy, copy in copies(l, slot):
            pl.when(reach(-dx, -dy))(copy.start)

    def arrive(l, slot):
        for dx, dy, copy in copies(l, slot):
            pl.when(reach(dx, dy))(copy.wait_recv)
            pl.when(reach(-dx, -dy))(copy.wait_send)

    def pair(name, *at):
        return tuple(R[name + h][at] if at else R[name + h][...] for h in ("h", "l"))

    def apply_step(l, k, slot):
        lev = levels[l]
        rows = lev.rows
        s, d, r, x, prod = (R[f"{n}{l}"] for n in ("s", "d", "r", "x", "prod"))
        exchange(l, slot, lambda c: s[...] * d[c])

        def near(c, _):
            prod[c] = dot3(pair(f"wo{l}", c), halves(R[f"work{l}"][c]))
            return 0

        def far(c, _):
            prod[c] += dot3(pair(f"wh{l}", c), halves(R[f"halo{l}"][slot, c]))
            return 0

        lax.fori_loop(0, 3, near, 0)
        arrive(l, slot)
        lax.fori_loop(0, 3, far, 0)

        def group(c, g):
            return prod[c, g * rows : (g + 1) * rows, :]

        zmat = [pair(f"z{l}", i) for i in range(5)]
        parts = [
            ((group(0, 0) + group(1, 2), 0), (group(0, 1), 1), (group(2, 2), 4)),
            ((group(1, 0) + group(0, 2), 0), (group(1, 1), 1), (group(2, 3), 4)),
            ((group(2, 0), 0), (group(2, 1), 2), (group(0, 3) + group(1, 3), 3)),
        ]
        c1 = R["coef"][l, 2 * k]
        c2 = R["coef"][l, 2 * k + 1]
        for c in range(3):
            total = None
            for val, z in parts[c]:
                one = dot3(halves(val), zmat[z])
                total = one if total is None else total + one
            res = r[c] - (s[...] * total + R[f"f{l}"][...] * d[c])
            r[c] = res
            new = c1 * d[c] + c2 * (R[f"dinv{l}"][c] * res)
            d[c] = new
            x[c] += new

    def move(l, slot, value, name, out):
        exchange(l, slot, value)
        arrive(l, slot)

        def one(c, _):
            flat = dot3(pair(name + "o"), halves(R[f"work{l}"][c]))
            flat += dot3(pair(name + "h"), halves(R[f"halo{l}"][slot, c]))
            out(c, dot3(halves(flat), pair(name + "z")))
            return 0

        lax.fori_loop(0, 3, one, 0)

    def start(l, c, b):
        first = R["coef"][l, 12] * (R[f"dinv{l}"][c] * b)
        R[f"r{l}"][c] = b
        R[f"d{l}"][c] = first
        R[f"x{l}"][c] = first

    def run(l):
        last = l == len(levels) - 1

        def body(k, _):
            slot = k % 2 if last else (k + k // 3) % 2
            apply_step(l, k, slot)
            if not last:

                @pl.when(k == DEG - 1)
                def _():
                    def down(c, val):
                        start(l + 1, c, (1.0 - R[f"f{l + 1}"][...]) * val)

                    def up(c, val):
                        step = (1.0 - R[f"f{l}"][...]) * val
                        R[f"d{l}"][c] = step
                        R[f"x{l}"][c] += step

                    move(l, 1, lambda c: (1.0 - R[f"f{l}"][...]) * R[f"r{l}"][c], f"rs{l}", down)
                    run(l + 1)
                    move(l + 1, 1, lambda c: R[f"x{l + 1}"][c], f"pr{l}", up)

            return 0

        lax.fori_loop(0, COARSE_DEG - 1 if last else 2 * DEG, body, 0)

    chebyshev_table(R["spectrum"], R["coef"])
    vecs, nz = levels[0].vecs, levels[0].nz
    for c in range(3):
        for v in range(vecs):
            R["r0"][c, :, v * nz : (v + 1) * nz] = R["modes"][v, c]
        start(0, c, R["r0"][c])
    run(0)
    for c in range(3):
        for v in range(vecs):
            R["out"][v, c] = R["x0"][c, :, v * nz : (v + 1) * nz]


def chebyshev_table(spectrum, coef):
    for l in range(3):
        low, top = spectrum[l, 0], spectrum[l, 1]
        center = 0.5 * (top + low)
        radius = 0.5 * (top - low)
        ratio = center / radius
        rho = 1.0 / ratio
        steps = []
        for _ in range(COARSE_DEG - 1):
            rho_next = 1.0 / (2.0 * ratio - rho)
            steps.append((rho_next * rho, 2.0 * rho_next / radius))
            rho = rho_next
        smooth = steps[: DEG - 1]
        flat = [(0.0, 0.0), (0.0, 1.0 / center)]
        picked = steps if l == 2 else smooth + flat + smooth
        for k, two in enumerate(picked):
            coef[l, 2 * k] = jnp.asarray(two[0], F32)
            coef[l, 2 * k + 1] = jnp.asarray(two[1], F32)
        coef[l, 12] = 1.0 / center


def local(modes, moduli, pinned, spectrum):
    vecs, _, nx, ny, nz = modes.shape
    levels = []
    names, args = [], []

    def add(name, value):
        names.append(name)
        args.append(value)

    for l, degree in enumerate(DEGREES):
        step = DEGREES[0] // degree
        levels.append(Level(degree, nx // step, ny // step, nz // step, vecs))
    add("spectrum", spectrum)
    add("modes", modes.reshape(vecs, 3, nx * ny, nz))
    for l, lev in enumerate(levels):
        step = DEGREES[0] // lev.p
        w = moduli[::step, ::step, ::step]
        f = pinned[::step, ::step, ::step].astype(F32)
        s = w * (1.0 - f)
        dinv = 1.0 / (s * s * lev.diagonal() + f)

        def spread(a, fill):
            a = a.reshape(a.shape[:-3] + (lev.own, lev.nz))
            a = jnp.concatenate([a] * vecs, -1)
            wide = [(0, 0)] * (a.ndim - 2)
            wide += [(0, lev.rows - lev.own), (0, lev.lanes - vecs * lev.nz)]
            return jnp.pad(a, wide, constant_values=fill)

        add(f"s{l}", spread(s, 0.0))
        add(f"f{l}", spread(f, 1.0))
        add(f"dinv{l}", spread(dinv, 1.0))
        mats = dict(zip((f"wo{l}", f"wh{l}", f"z{l}"), lev.operator()))
        if l + 1 < len(levels):
            keys = [f"{a}{l}{b}" for a in ("rs", "pr") for b in "ohz"]
            mats.update(zip(keys, transfer(lev, levels[l + 1])))
        for key, mat in mats.items():
            for tag, half in zip("hl", split(mat)):
                add(key + tag, jnp.asarray(half))

    specs = [
        pl.BlockSpec(memory_space=pltpu.SMEM if n == "spectrum" else pltpu.VMEM) for n in names
    ]
    scratch = []
    all_names = names + ["out"]

    def temp(name, what):
        all_names.append(name)
        scratch.append(what)

    temp("coef", pltpu.SMEM((3, 13), F32))
    for l, lev in enumerate(levels):
        field = (3, lev.rows, lev.lanes)
        for n in ("r", "d", "x", "work"):
            temp(f"{n}{l}", pltpu.VMEM(field, F32))
        temp(f"prod{l}", pltpu.VMEM((3, 4 * lev.rows, lev.lanes), F32))
        temp(f"send{l}", pltpu.VMEM((3, lev.halo, lev.lanes), F32))
        temp(f"halo{l}", pltpu.VMEM((2, 3, lev.halo, lev.lanes), F32))
        temp(f"ssem{l}", pltpu.SemaphoreType.DMA((len(DIRS),)))
        temp(f"rsem{l}", pltpu.SemaphoreType.DMA((2, len(DIRS))))
    out = pl.pallas_call(
        functools.partial(kernel, levels, all_names),
        out_shape=jax.ShapeDtypeStruct((vecs, 3, nx * ny, nz), F32),
        in_specs=specs,
        out_specs=pl.BlockSpec(memory_space=pltpu.VMEM),
        scratch_shapes=scratch,
        compiler_params=pltpu.CompilerParams(
            collective_id=0, has_side_effects=True, vmem_limit_bytes=60 * 1024 * 1024
        ),
    )(*args)
    return out.reshape(modes.shape)


def solution(mesh):
    placed = (P(None, None, "gx", "gy", None), P("gx", "gy", None), P("gx", "gy", None), P())
    return jax.shard_map(
        local,
        mesh=mesh,
        in_specs=placed,
        out_specs=P(None, None, "gx", "gy", None),
        check_vma=False,
    )
```

time: 598 us -> 168 us (0.28)
  the two profiles are of different devices: /device:TPU:1 before, /device:TPU:19 now
where the time goes in v1:
time: 168 us; the launch traced here: 167 us
  Pallas kernels  141 us (84%)
  local copies, waits for them, and re-layouts  19.1 us (11%)
  other arithmetic  6.32 us (4%)
    pallas_call x1, Pallas kernels, local(): pl.pallas_call(functools.partial(kernel, levels, all_names), out_shape=ja...  141 us
    another operation x11, local copies, waits for them, and re-layouts  6.74 us
    slice x2, local copies, waits for them, and re-layouts, local(): w = moduli[::step, ::step, ::step]  4.49 us
    slice x2, local copies, waits for them, and re-layouts, local(): f = pinned[::step, ::step, ::step].astype(F32)  4.48 us
    concatenate x6, other arithmetic, spread(): a = jnp.concatenate([a] * vecs, -1)  4.4 us

profile of v1, /device:TPU:19, one launch (start us, length us, event | category | flops | bytes accessed | tf_op | source)
XLA Modules:
  0.0 166.9 jit_solution(14766997475662711803)
XLA Ops:
  0.0 0.0 copy-start.1
  0.0 0.0 copy-start
  0.0 1.4 copy.50.refs_0_
  1.4 1.7 %slice.15 = s32[3,4,32]{2,1,0:T(4,128)S(1)} slice(s32[12,16,128]{2,1,0:T(8,128)} %param.51), slice={[0:12:4], [0:16:4], [0:128:4]} | slice | bytes 3072 | tf_op jit(solution)/shard_map/slice | solution.py:437
  3.2 1.8 %slice.14 = f32[3,4,32]{2,1,0:T(4,128)S(1)} slice(f32[12,16,128]{2,1,0:T(8,128)} %param.50), slice={[0:12:4], [0:16:4], [0:128:4]} | slice | bytes 3072 | tf_op jit(solution)/shard_map/slice | solution.py:436
  5.0 0.7 select_maximum_fusion.1
  5.7 0.7 select_maximum_fusion.refs_46_
  6.4 2.7 %slice.13 = s32[6,8,64]{2,1,0:T(8,128)S(1)} slice(s32[12,16,128]{2,1,0:T(8,128)} %param.51), slice={[0:12:2], [0:16:2], [0:128:2]} | slice | bytes 24576 | tf_op jit(solution)/shard_map/slice | solution.py:437
  9.1 2.7 %slice.12 = f32[6,8,64]{2,1,0:T(8,128)S(1)} slice(f32[12,16,128]{2,1,0:T(8,128)} %param.50), slice={[0:12:2], [0:16:2], [0:128:2]} | slice | bytes 24576 | tf_op jit(solution)/shard_map/slice | solution.py:436
  11.9 0.9 divide_bitcast_fusion
  12.8 0.7 pad_maximum_fusion.3.refs_25_
  13.5 0.7 pad_maximum_fusion.4
  14.2 0.9 convert_element_type.9
  15.1 0.0 copy-done
  15.1 0.0 copy-done.2
  15.1 0.0 copy-done.1
  15.2 0.1 add_divide_fusion
  15.2 0.9 pad_maximum_fusion.refs_4_
  16.1 0.8 pad_maximum_fusion.1
  16.8 0.6 jit_solution_.40.refs_35_
  17.4 0.6 jit_solution_.39.refs_33_
  18.0 0.6 jit_solution_.42.refs_41_
  18.6 0.6 jit_solution_.41.refs_39_
  19.2 0.6 jit_solution_.34.refs_14_
  19.8 0.6 jit_solution_.33.refs_12_
  20.5 0.6 call_exported.0.refs_37_.refs_43_
  21.1 0.6 jit_solution_.37.refs_20_
  21.7 0.6 jit_solution_.36.refs_18_
  22.3 0.6 jit_solution_.38.refs_22_
  22.9 0.6 jit_solution_.35.refs_16_
  23.6 141.4 %shard_map.451 = f32[2,3,192,128]{3,2,1,0:T(8,128)} custom-call(f32[3,2]{1,0:T(4,128)} %copy.50.refs_0_, f32[2,3,192,128]{3,2,1,0:T(8,128)} %bitcast.14, f32[192,256]{1,0:T(8,128)} %get-tuple-element.13.refs_2_, f32[192,256]{1,0:T(8,128)} %get-tuple-element.14.refs_3_, f32[3,192,256]{2,1,0:T(8,128)} %pad_maximum_fusion.refs_4_, ...), custom_call_target="tpu_custom_call" | custom-call | tf_op jit(solution)/shard_map/pallas_call | solution.py:479
  165.0 1.9 %copy.52 = f32[2,3,12,16,128]{4,3,2,1,0:T(8,128)} copy(f32[2,3,12,16,128]{4,3,2,1,0:T(8,128)} %bitcast.11) | data formatting | bytes 1179648
  (10 shorter events, 0.1 us)
Async XLA Ops:
  0.0 15.1 %copy-start.1 = (f32[3,12,16,128]{3,2,1,0:T(8,128)S(1)}, f32[3,12,16,128]{3,2,1,0:T(8,128)}, u32[]{:S(2)}) copy-start(f32[3,12,16,128]{3,2,1,0:T(8,128)} %constant.46.clone) | copy-start | bytes 884740
  0.0 15.1 %copy-start = (s32[12,16,128]{2,1,0:T(8,128)S(1)}, s32[12,16,128]{2,1,0:T(8,128)}, u32[]{:S(2)}) copy-start(s32[12,16,128]{2,1,0:T(8,128)} %param.51) | copy-start | bytes 294916
  0.0 15.1 %copy-start.2 = (f32[12,16,128]{2,1,0:T(8,128)S(1)}, f32[12,16,128]{2,1,0:T(8,128)}, u32[]{:S(2)}) copy-start(f32[12,16,128]{2,1,0:T(8,128)} %param.50) | copy-start | bytes 294916

commit v2 on v1

--- a/solution.py
+++ b/solution.py
@@ -84,6 +84,7 @@
         self.own = nx * ny
         self.rows = up8(self.own)
         self.lanes = -(-vecs * nz // 128) * 128
+        self.blocked = nz % 128 == 0
         self.pos = [(x, y) for x in range(nx) for y in range(ny)]
         self.pos += [None] * (self.rows - self.own)
         self.blocks = []
@@ -142,7 +143,8 @@
                 ]
             )
 
-        line = [self.lift_z(dense(e, self.nz)[:, self.p : self.p + self.nz], self) for e in t]
+        line = [dense(e, self.nz)[:, self.p : self.p + self.nz] for e in t]
+        line = [e.T if self.blocked else self.lift_z(e, self) for e in line]
         z_ops = np.stack([line[0], MU_SHEAR * line[1], big * line[1], line[2], line[3]])
         return build(self.pos), build(self.halo_pos), z_ops
 
@@ -158,15 +160,29 @@
         def center(table, count):
             return table[np.arange(count) % self.p, self.p]
 
-        m = [center(t[0], n) for n in (self.nx, self.ny, self.nz)]
-        k = [center(t[1], n) for n in (self.nx, self.ny, self.nz)]
-        out = np.zeros((3, self.nx, self.ny, self.nz))
+        m_x, m_y, m_z = [center(t[0], n) for n in (self.nx, self.ny, self.nz)]
+        k_x, k_y, k_z = [center(t[1], n) for n in (self.nx, self.ny, self.nz)]
+        rows = np.zeros((self.rows, 128), np.float32)
         for c in range(3):
-            for e in range(3):
-                coef = MU_SHEAR + (LAMBDA_BULK + MU_SHEAR) * (c == e)
-                f = [k[i] if i == e else m[i] for i in range(3)]
-                out[c] += coef * f[0][:, None, None] * f[1][None, :, None] * f[2][None, None, :]
-        return out.astype(np.float32)
+            coef = [MU_SHEAR + (LAMBDA_BULK + MU_SHEAR) * (c == e) for e in range(3)]
+            plane = coef[0] * np.outer(k_x, m_y) + coef[1] * np.outer(m_x, k_y)
+            rows[: self.own, c] = plane.ravel()
+            rows[: self.own, 3 + c] = (coef[2] * np.outer(m_x, m_y)).ravel()
+        lanes = np.zeros((8, self.lanes), np.float32)
+        lanes[0, : self.vecs * self.nz] = np.tile(m_z, self.vecs)
+        lanes[1, : self.vecs * self.nz] = np.tile(k_z, self.vecs)
+        return rows, lanes
+
+    def sample(self, top):
+        step = top.p // self.p
+        sel_x = np.zeros((self.rows, top.own))
+        for i, (x, y) in enumerate(self.pos[: self.own]):
+            sel_x[i, x * step * top.ny + y * step] = 1
+        sel_z = np.zeros((top.nz, self.lanes))
+        for v in range(self.vecs):
+            for z in range(self.nz):
+                sel_z[z * step, v * self.nz + z] = 1
+        return sel_x, sel_z
 
 
 def prolong_dense(table, fine_n, lead):
@@ -243,6 +259,29 @@
     def device(dx, dy):
         return (jnp.clip(me_x + dx, 0, gx_n - 1), jnp.clip(me_y + dy, 0, gy_n - 1))
 
+    top = levels[0]
+    vecs, nz = top.vecs, top.nz
+    if top.blocked:
+        for h in "hl":
+            R[f"z0{h}"][...] = jnp.zeros_like(R[f"z0{h}"])
+    moves = [(R["moduli_in"], R["moduli"]), (R["pinned_in"], R["pinned"])]
+    for v in range(vecs):
+        moves.append((R["modes"].at[v], R["r0"].at[:, :, pl.ds(v * nz, nz)]))
+    for name in names:
+        if name.endswith("_in") and name[:-3] not in ("moduli", "pinned"):
+            src, dst = R[name], R[name[:-3]]
+            if name[:2] == "z0" and top.blocked:
+                for v in range(vecs):
+                    at = pl.ds(v * nz, nz)
+                    moves.append((src, dst.at[:, at, at]))
+            else:
+                moves.append((src, dst))
+    moves = [
+        pltpu.make_async_copy(src, dst, R["lsem"].at[i]) for i, (src, dst) in enumerate(moves)
+    ]
+    for one in moves:
+        one.start()
+    chebyshev_table(R["spectrum"], R["coef"])
     for l, lev in enumerate(levels):
         R[f"halo{l}"][...] = jnp.zeros_like(R[f"halo{l}"])
         R[f"send{l}"][...] = jnp.zeros_like(R[f"send{l}"])
@@ -261,8 +300,10 @@
     ]
     pl.semaphore_wait(barrier, around[0] * around[1] - 1)
 
-    def copies(l, slot):
+    def copies(l, slot, side):
         for i, (dx, dy) in enumerate(DIRS):
+            if side and -side in (dx, dy):
+                continue
             start, size, _ = levels[l].blocks[i]
             yield (
                 dx,
@@ -277,7 +318,7 @@
                 ),
             )
 
-    def exchange(l, slot, value):
+    def exchange(l, slot, value, side=0):
         lev = levels[l]
         work, send = R[f"work{l}"], R[f"send{l}"]
 
@@ -289,11 +330,11 @@
             return 0
 
         lax.fori_loop(0, 3, stage, 0)
-        for dx, dy, copy in copies(l, slot):
+        for dx, dy, copy in copies(l, slot, side):
             pl.when(reach(-dx, -dy))(copy.start)
 
-    def arrive(l, slot):
-        for dx, dy, copy in copies(l, slot):
+    def arrive(l, slot, side=0):
+        for dx, dy, copy in copies(l, slot, side):
             pl.when(reach(dx, dy))(copy.wait_recv)
             pl.when(reach(-dx, -dy))(copy.wait_send)
 
@@ -340,9 +381,9 @@
             d[c] = new
             x[c] += new
 
-    def move(l, slot, value, name, out):
-        exchange(l, slot, value)
-        arrive(l, slot)
+    def move(l, slot, value, name, out, side):
+        exchange(l, slot, value, side)
+        arrive(l, slot, side)
 
         def one(c, _):
             flat = dot3(pair(name + "o"), halves(R[f"work{l}"][c]))
@@ -376,24 +417,57 @@
                         R[f"d{l}"][c] = step
                         R[f"x{l}"][c] += step
 
-                    move(l, 1, lambda c: (1.0 - R[f"f{l}"][...]) * R[f"r{l}"][c], f"rs{l}", down)
+                    move(l, 1, lambda c: (1.0 - R[f"f{l}"][...]) * R[f"r{l}"][c], f"rs{l}", down, -1)
                     run(l + 1)
-                    move(l + 1, 1, lambda c: R[f"x{l + 1}"][c], f"pr{l}", up)
+                    move(l + 1, 1, lambda c: R[f"x{l + 1}"][c], f"pr{l}", up, 1)
 
             return 0
 
         lax.fori_loop(0, COARSE_DEG - 1 if last else 2 * DEG, body, 0)
 
-    chebyshev_table(R["spectrum"], R["coef"])
-    vecs, nz = levels[0].vecs, levels[0].nz
+    for one in moves:
+        one.wait()
+    free = 1.0 - R["pinned"][...].astype(F32)
+    scale = R["moduli"][...] * free
+
+    def times01(a, b):
+        return lax.dot_general(a, b, (((1,), (0,)), ((), ())), preferred_element_type=F32)
+
+    def thirds(value):
+        hi, lo = halves(value)
+        rest = value - hi.astype(F32) - lo.astype(F32)
+        return hi, lo, rest.astype(BF16)
+
+    for l, lev in enumerate(levels):
+        if l == 0 and lev.blocked:
+            for v in range(vecs):
+                at = pl.ds(v * nz, nz)
+                R["s0"][:, at] = scale
+                R["f0"][:, at] = 1.0 - free
+        else:
+            sel_x, sel_z = R[f"sx{l}"][...], R[f"sz{l}"][...]
+            picked = sum(times01(sel_x, part) for part in thirds(scale))
+            R[f"s{l}"][...] = sum(times01(part, sel_z) for part in thirds(picked))
+            picked = times01(sel_x, free.astype(BF16))
+            R[f"f{l}"][...] = 1.0 - times01(picked.astype(BF16), sel_z)
+        square = R[f"s{l}"][...] * R[f"s{l}"][...]
+        m_z, k_z = R[f"kl{l}"][0:1, :], R[f"kl{l}"][1:2, :]
+        for c in range(3):
+            kd = R[f"kr{l}"][:, c : c + 1] * m_z + R[f"kr{l}"][:, 3 + c : 4 + c] * k_z
+            R[f"dinv{l}"][c] = 1.0 / (square * kd + R[f"f{l}"][...])
     for c in range(3):
-        for v in range(vecs):
-            R["r0"][c, :, v * nz : (v + 1) * nz] = R["modes"][v, c]
         start(0, c, R["r0"][c])
     run(0)
-    for c in range(3):
-        for v in range(vecs):
-            R["out"][v, c] = R["x0"][c, :, v * nz : (v + 1) * nz]
+    backs = [
+        pltpu.make_async_copy(
+            R["x0"].at[:, :, pl.ds(v * nz, nz)], R["out"].at[v], R["lsem"].at[v]
+        )
+        for v in range(vecs)
+    ]
+    for one in backs:
+        one.start()
+    for one in backs:
+        one.wait()
 
 
 def chebyshev_table(spectrum, coef):
@@ -431,33 +505,24 @@
         levels.append(Level(degree, nx // step, ny // step, nz // step, vecs))
     add("spectrum", spectrum)
     add("modes", modes.reshape(vecs, 3, nx * ny, nz))
+    add("moduli_in", moduli.reshape(nx * ny, nz))
+    add("pinned_in", pinned.reshape(nx * ny, nz))
     for l, lev in enumerate(levels):
-        step = DEGREES[0] // lev.p
-        w = moduli[::step, ::step, ::step]
-        f = pinned[::step, ::step, ::step].astype(F32)
-        s = w * (1.0 - f)
-        dinv = 1.0 / (s * s * lev.diagonal() + f)
-
-        def spread(a, fill):
-            a = a.reshape(a.shape[:-3] + (lev.own, lev.nz))
-            a = jnp.concatenate([a] * vecs, -1)
-            wide = [(0, 0)] * (a.ndim - 2)
-            wide += [(0, lev.rows - lev.own), (0, lev.lanes - vecs * lev.nz)]
-            return jnp.pad(a, wide, constant_values=fill)
-
-        add(f"s{l}", spread(s, 0.0))
-        add(f"f{l}", spread(f, 1.0))
-        add(f"dinv{l}", spread(dinv, 1.0))
         mats = dict(zip((f"wo{l}", f"wh{l}", f"z{l}"), lev.operator()))
         if l + 1 < len(levels):
             keys = [f"{a}{l}{b}" for a in ("rs", "pr") for b in "ohz"]
             mats.update(zip(keys, transfer(lev, levels[l + 1])))
         for key, mat in mats.items():
             for tag, half in zip("hl", split(mat)):
-                add(key + tag, jnp.asarray(half))
+                add(key + tag + "_in", jnp.asarray(half))
+        for key, mat in zip(("kr", "kl"), lev.diagonal()):
+            add(f"{key}{l}_in", jnp.asarray(mat))
+        if l or not lev.blocked:
+            for key, mat in zip(("sx", "sz"), lev.sample(levels[0])):
+                add(f"{key}{l}_in", jnp.asarray(mat.astype(BF16)))
 
     specs = [
-        pl.BlockSpec(memory_space=pltpu.SMEM if n == "spectrum" else pltpu.VMEM) for n in names
+        pl.BlockSpec(memory_space=pltpu.SMEM if n == "spectrum" else pl.ANY) for n in names
     ]
     scratch = []
     all_names = names + ["out"]
@@ -467,9 +532,18 @@
         scratch.append(what)
 
     temp("coef", pltpu.SMEM((3, 13), F32))
+    temp("lsem", pltpu.SemaphoreType.DMA((len(names) + 2 * vecs,)))
+    for name, value in zip(names, args):
+        if name.endswith("_in"):
+            shape = value.shape
+            if name[:2] == "z0" and levels[0].blocked:
+                shape = (shape[0], levels[0].lanes, levels[0].lanes)
+            temp(name[:-3], pltpu.VMEM(shape, value.dtype))
     for l, lev in enumerate(levels):
         field = (3, lev.rows, lev.lanes)
-        for n in ("r", "d", "x", "work"):
+        for n in ("s", "f"):
+            temp(f"{n}{l}", pltpu.VMEM(field[1:], F32))
+        for n in ("r", "d", "x", "work", "dinv"):
             temp(f"{n}{l}", pltpu.VMEM(field, F32))
         temp(f"prod{l}", pltpu.VMEM((3, 4 * lev.rows, lev.lanes), F32))
         temp(f"send{l}", pltpu.VMEM((3, lev.halo, lev.lanes), F32))
@@ -480,7 +554,7 @@
         functools.partial(kernel, levels, all_names),
         out_shape=jax.ShapeDtypeStruct((vecs, 3, nx * ny, nz), F32),
         in_specs=specs,
-        out_specs=pl.BlockSpec(memory_space=pltpu.VMEM),
+        out_specs=pl.BlockSpec(memory_space=pl.ANY),
         scratch_shapes=scratch,
         compiler_params=pltpu.CompilerParams(
             collective_id=0, has_side_effects=True, vmem_limit_bytes=60 * 1024 * 1024

time: 168 us -> 148 us (0.88)
  local copies, waits for them, and re-layouts: 19.1 us -> 9.98 us
  other arithmetic: 6.32 us -> 0 us
  Pallas kernels: 141 us -> 136 us
    slice x4 -> x0, local copies, waits for them, and re-layouts: 8.97 us -> none  [the longest x2 4.49 us: local(): w = moduli[::step, ::step, ::step]]
    pallas_call x1, Pallas kernels: 141 us -> 136 us  [local(): pl.pallas_call(functools.partial(kernel, levels, all_names), out_shape=ja...]
    concatenate x6 -> x0, other arithmetic: 4.4 us -> none  [spread(): a = jnp.concatenate([a] * vecs, -1)]
where the time goes in v2:
time: 148 us; the launch traced here: 146 us
  Pallas kernels  136 us (92%)
  local copies, waits for them, and re-layouts  9.98 us (7%)
    pallas_call x1, Pallas kernels, local(): pl.pallas_call(functools.partial(kernel, levels, all_names), out_shape=ja...  136 us
    another operation x11, local copies, waits for them, and re-layouts  6.7 us
    unnamed x2, local copies, waits for them, and re-layouts  3.28 us

profile of v2, /device:TPU:19, one launch (start us, length us, event | category | flops | bytes accessed | tf_op | source)
XLA Modules:
  0.0 145.6 jit_solution(14228341605715265744)
XLA Ops:
  0.0 1.3 copy.57.refs_0_
  1.3 0.6 jit_solution_.37.refs_33_
  1.9 0.6 jit_solution_.36.refs_31_
  2.5 0.6 jit_solution_.39.refs_39_
  3.1 0.6 jit_solution_.38.refs_37_
  3.7 0.6 jit_solution_.31.refs_13_
  4.3 0.6 jit_solution_.30.refs_11_
  4.9 0.6 call_exported.0.refs_35_.refs_41_
  5.5 0.6 jit_solution_.34.refs_19_
  6.2 0.6 jit_solution_.33.refs_17_
  6.8 0.6 jit_solution_.35.refs_21_
  7.4 0.6 jit_solution_.32.refs_15_
  8.0 135.6 %shard_map.514 = f32[2,3,192,128]{3,2,1,0:T(8,128)} custom-call(f32[3,2]{1,0:T(4,128)} %copy.57.refs_0_, f32[2,3,192,128]{3,2,1,0:T(8,128)} %bitcast.5, f32[192,128]{1,0:T(8,128)} %bitcast.6, s32[192,128]{1,0:T(8,128)} %bitcast.7, bf16[3,768,192]{2,1,0:T(8,128)(2,1)} %constant.102.clone.refs_4_, bf16[3,768,192]{2,1,0:T(8,128)(2,1)} %constant.103.clone.refs_5_, ...), custom_call_target="tpu_custom_call" | custom-call | tf_op jit(solution)/shard_map/pallas_call | solution.py:553
  143.7 1.9 %copy.59 = f32[2,3,12,16,128]{4,3,2,1,0:T(8,128)} copy(f32[2,3,12,16,128]{4,3,2,1,0:T(8,128)} %bitcast.4) | data formatting | bytes 1179648
